TPU v7x, 32 devices: a whole 2x2x4 slice. The times are simulated.
32 devices in a mesh: occ: 4 (over y, core), vir: 8 (over z, x).
Axes of the slice: x: 2, y: 2, z: 4, core: 2. Of those that a mesh axis runs over, the one named last changes fastest.
Arguments:
- amplitudes: bfloat16 [2048, 4096], P('occ', 'vir'), may hold values from -6 to 6
- hole_integrals: bfloat16 [2048, 2048], P('occ'), may hold values from -0.375 to 0.375
- particle_integrals: bfloat16 [4096, 4096], P('vir'), may hold values from -0.375 to 0.375
- occ_irrep: int32 [32], replicated, may hold values from 0 to 7
- vir_irrep: int32 [64], replicated, may hold values from 0 to 7
- occ_energy: float32 [2048], P('occ'), may hold values from -1.5 to -0.5
- vir_energy: float32 [4096], P('vir'), may hold values from 0.5 to 2.5
Outputs:
- update: float32 [4096, 2048], P('vir', 'occ')
All inputs are finite; a program needn't handle non-finite values.
Results may differ from a plain program's by a relative error of at most 0.0003.
Values may be sent and summed in bfloat16 or wider, within the bound.
A program may use at most 128 MiB of HBM per device.

v0:
```python
import functools

import jax
import jax.numpy as jnp
from jax import lax
from jax.experimental import pallas as pl
from jax.experimental.pallas import tpu as pltpu
from jax.sharding import PartitionSpec as P

TILE = 64
CORES = 2
LINES = 4
ROWS = 4
HALVES = 2
TOP = 32000.0
MESH = pl.DeviceIdType.MESH
ORDER = (
    ("t", 0), ("v", 0, 0), ("v", 0, 1), ("t", 1), ("v", 1, 0), ("t", 2), ("t", 3), ("v", 1, 1),
    ("v", 2, 0), ("v", 2, 1), ("v", 3, 0), ("v", 3, 1),
)


def kernel(
    width, groups, amp, hole, slab, occ_irrep, vir_irrep, occ_e, vir_e, out,
    occ_tags, vir_tags, occ_labels, vir_labels, occ_row, vir_row,
    t_all, v_all, v_masked, v_send, cols_all, hole_all, acc, tmp, box_out, scale_out, box_in, scale_in, result,
    t_send, t_sem, v_sends, v_sem, relay_send, pair_send, pair_sem,
    box_send, box_sem, scale_send, scale_sem, local_sem, own_sem, load_sem, out_sem,
):
    p_own, q_own = amp.shape
    o, v = lax.axis_index("occ"), lax.axis_index("vir")
    c = lax.rem(o, CORES)
    z, x = v // width, lax.rem(v, width)
    occ_size = groups * CORES
    partner = o + 1 - 2 * c
    half = z // 2
    mid = lax.rem(z + half, 2)
    mate, far, near = z + 1 - 2 * lax.rem(z, 2), 3 * (1 - half), 2 - half
    owner = [mid * mate + (1 - mid) * far, mid * far + (1 - mid) * near, mid * near + (1 - mid) * mate, z]
    target = [mate, mid * far + (1 - mid) * mate, mid * near + (1 - mid) * mate]
    box = [2 * (1 - mid), mid + 3 * (1 - mid), mid]
    is_mid = mid == 1
    rows, cols, share = p_own // ROWS, q_own // HALVES, q_own // CORES
    tiles = q_own // TILE
    others = range(1, width)

    def xdev(k):
        return (o, z * width + lax.rem(x + k, width))

    def remote(src, dst, send, recv, device):
        return pltpu.make_async_remote_copy(
            src_ref=src, dst_ref=dst, send_sem=send, recv_sem=recv, device_id=device, device_id_type=MESH
        )

    def landed(ref, sem):
        pltpu.make_async_copy(ref, ref, sem).wait()

    barrier = pltpu.get_barrier_semaphore()
    peers = [(lax.rem(o + d, occ_size), v) for d in range(1, occ_size)]
    peers += [xdev(k) for k in others] + [(o, mate * width + x), (o, near * width + x)]
    for peer in peers:
        pl.semaphore_signal(barrier, inc=1, device_id=peer, device_id_type=MESH)

    loads = {}

    def load(name, src, dst, sem):
        loads[name] = pltpu.make_async_copy(src, dst, sem)
        loads[name].start()

    def columns(zz, xx):
        return pl.ds(pl.multiple_of((zz * width + xx) * q_own, q_own), q_own)

    load("amp", amp, t_all.at[:, pl.ds(0, q_own)], load_sem.at[0])
    for j in range(LINES):
        for k in others:
            load(
                ("send", j, k),
                slab.at[pl.ds(pl.multiple_of(c * share, share), share), columns(owner[j], lax.rem(x + k, width))],
                v_send.at[j, k - 1], local_sem.at[j, k - 1],
            )
        load(("own", j), slab.at[:, columns(owner[j], x)], v_all.at[j, pl.ds(0, q_own), :], own_sem.at[j])
    load("occ_tags", occ_irrep, occ_tags, load_sem.at[1])
    load("vir_tags", vir_irrep, vir_tags, load_sem.at[2])
    load("occ_row", occ_e, occ_row, load_sem.at[3])
    load("vir_row", vir_e, vir_row, load_sem.at[4])
    load("hole", hole, hole_all, load_sem.at[5])

    pl.semaphore_wait(barrier, len(peers) - 1 + 2 * mid)

    def t_copy(i, k):
        at = pl.ds(i * rows, rows)
        return remote(
            t_all.at[at, pl.ds(0, q_own)], t_all.at[at, pl.ds((width - k) * q_own, q_own)],
            t_send.at[k - 1, i], t_sem.at[width - k - 1, i], xdev(k),
        )

    def v_piece(j, h, d, core):
        return v_all.at[
            j, pl.ds(pl.multiple_of(d * q_own + core * share, share), share), pl.ds(h * cols, cols)
        ]

    def v_copy(j, h, k):
        return remote(
            v_send.at[j, k - 1, :, pl.ds(h * cols, cols)], v_piece(j, h, width - k, c),
            v_sends.at[k - 1, j, h], v_sem.at[width - k - 1, j, h, c], xdev(k),
        )

    def relay_copy(j, h, d):
        piece = v_piece(j, h, d, c)
        return remote(piece, piece, relay_send.at[d - 1, j, h], v_sem.at[d - 1, j, h, c], (partner, v))

    def pair_copy(d):
        return remote(
            t_all.at[:, pl.ds(0, q_own)], cols_all.at[pl.ds(pl.multiple_of(o * p_own, p_own), p_own), :],
            pair_send.at[d - 1], pair_sem.at[o], (lax.rem(o + d, occ_size), v),
        )

    loads["amp"].wait()
    fetched = set()
    for step in ORDER:
        if step[0] == "t":
            for k in others:
                t_copy(step[1], k).start()
            if step[1] == 0:
                for d in range(1, occ_size):
                    pair_copy(d).start()
                load("pairs", amp, cols_all.at[pl.ds(pl.multiple_of(o * p_own, p_own), p_own), :], load_sem.at[6])
        else:
            for k in others:
                if (step[1], k) not in fetched:
                    fetched.add((step[1], k))
                    loads["send", step[1], k].wait()
                v_copy(step[1], step[2], k).start()

    loads["occ_tags"].wait()
    loads["vir_tags"].wait()
    low = lax.broadcasted_iota(jnp.int32, (1, 2 * TILE), 1) < TILE
    for j in range(LINES):
        base = (owner[j] * width + x) * tiles

        @pl.loop(0, tiles // 2)
        def _(i):
            at = pl.ds(pl.multiple_of(i * 2 * TILE, 2 * TILE), 2 * TILE)
            vir_labels[j, :, at] = jnp.where(low, vir_tags[base + 2 * i], vir_tags[base + 2 * i + 1])

    @pl.loop(0, occ_tags.shape[0] // 2)
    def _(i):
        at = pl.ds(pl.multiple_of(i * 2 * TILE, 2 * TILE), 2 * TILE)
        occ_labels[:, at] = jnp.where(low, occ_tags[2 * i], occ_tags[2 * i + 1])

    def mask(j, d, at):
        first = (z * width + lax.rem(x + d, width)) * tiles
        labels = vir_labels[j, :, at]

        @pl.loop(0, tiles)
        def _(i):
            part = pl.ds(pl.multiple_of(d * q_own + i * TILE, TILE), TILE)
            keep = (labels == vir_tags[first + i]).astype(jnp.float32).astype(jnp.bfloat16)
            v_masked[j, part, at] = v_all[j, part, at] * keep

    everything = pl.ds(0, q_own)
    loads["own", 0].wait()
    mask(0, 0, everything)

    loads["hole"].wait()

    @pl.loop(0, p_own // TILE)
    def _(i):
        at = pl.ds(pl.multiple_of(i * TILE, TILE), TILE)
        keep = (occ_labels[...] == occ_tags[o * (p_own // TILE) + i]).astype(jnp.float32).astype(jnp.bfloat16)
        hole_all[at, :] = hole_all[at, :] * keep

    def box_copies(j, h, i):
        at, there = pl.ds(pl.multiple_of(i * rows, rows), rows), pl.ds(h * cols, cols)
        device = (o, target[j] * width + x)
        return (
            remote(
                box_out.at[j, at, there], box_in.at[box[j], at, there],
                box_send.at[j, h, i], box_sem.at[box[j], h, i], device,
            ),
            remote(
                scale_out.at[j * ROWS + i, :, there], scale_in.at[box[j] * ROWS + i, :, there],
                scale_send.at[j, h, i], scale_sem.at[box[j], h, i], device,
            ),
        )

    def arrived(b, h, i):
        at, there = pl.ds(pl.multiple_of(i * rows, rows), rows), pl.ds(h * cols, cols)
        landed(box_in.at[b, at, there], box_sem.at[b, h, i])
        landed(scale_in.at[b * ROWS + i, :, there], scale_sem.at[b, h, i])
        return box_in[b, at, there].astype(jnp.float32) * scale_in[b * ROWS + i, :, there]

    def unit(j, h, i):
        at, there = pl.ds(pl.multiple_of(i * rows, rows), rows), pl.ds(h * cols, cols)
        part = jnp.dot(t_all[at, :], v_masked[j, :, there], preferred_element_type=jnp.float32)
        if j == LINES - 1:
            acc[at, there] += part
            return
        if j > 0:
            tmp[...] = part

            @pl.when(is_mid)
            def _():
                tmp[...] += arrived(j + 1, h, i)

            part = tmp[...]
        most = jnp.maximum(jnp.max(jnp.abs(part), axis=0, keepdims=True), 1e-30)
        box_out[j, at, there] = jnp.round(part * (TOP / most)).astype(jnp.int32).astype(jnp.int16)
        scale_out[j * ROWS + i, :, there] = most * (1.0 / TOP)
        for copy in box_copies(j, h, i):
            copy.start()

    have_t, have_v = 0, []
    for step in ORDER:
        if step[0] == "t":
            i = step[1]
            for d in others:
                landed(t_all.at[pl.ds(i * rows, rows), pl.ds(d * q_own, q_own)], t_sem.at[d - 1, i])
            have_t = i + 1
            for j, h in have_v:
                unit(j, h, i)
        else:
            j, h = step[1:]
            for d in others:
                landed(v_piece(j, h, d, c), v_sem.at[d - 1, j, h, c])
                relay_copy(j, h, d).start()
            if h == 0 and j > 0:
                loads["own", j].wait()
                mask(j, 0, everything)
            if j == LINES - 1 and h == 0:
                loads["pairs"].wait()
                for d in range(1, occ_size):
                    oo = lax.rem(o + d, occ_size)
                    landed(cols_all.at[pl.ds(pl.multiple_of(oo * p_own, p_own), p_own), :], pair_sem.at[oo])

                @pl.loop(0, ROWS)
                def _(i):
                    at = pl.ds(pl.multiple_of(i * rows, rows), rows)
                    acc[at, :] = jnp.dot(hole_all[at, :], cols_all[...], preferred_element_type=jnp.float32)

            for d in others:
                landed(v_piece(j, h, d, 1 - c), v_sem.at[d - 1, j, h, 1 - c])
                mask(j, d, pl.ds(h * cols, cols))
            have_v.append((j, h))
            if have_t == ROWS:

                @pl.loop(0, ROWS)
                def _(i):
                    unit(j, h, i)
            else:
                for i in range(have_t):
                    unit(j, h, i)

    loads["occ_row"].wait()
    loads["vir_row"].wait()

    def out_copy(h, i):
        at, there = pl.ds(pl.multiple_of(i * rows, rows), rows), pl.ds(h * cols, cols)
        return pltpu.make_async_copy(result.at[there, at], out.at[there, at], out_sem.at[h, i])

    for h in range(HALVES):
        there = pl.ds(h * cols, cols)
        column = jnp.broadcast_to(vir_row[:, there], (rows, cols)).T

        @pl.loop(0, ROWS)
        def _(i):
            at = pl.ds(pl.multiple_of(i * rows, rows), rows)
            total = acc[at, there] + arrived(1, h, i)
            total = total + arrived(0, h, i)
            result[there, at] = total.T / (column - occ_row[:, at])
            out_copy(h, i).start()

    for h in range(HALVES):

        @pl.loop(0, ROWS)
        def _(i):
            out_copy(h, i).wait()
            for j in range(LINES - 1):
                for copy in box_copies(j, h, i):
                    copy.wait_send()

    for d in range(1, occ_size):
        pair_copy(d).wait_send()
    for k in others:
        for i in range(ROWS):
            t_copy(i, k).wait_send()
        for j in range(LINES):
            for h in range(HALVES):
                v_copy(j, h, k).wait_send()
                relay_copy(j, h, k).wait_send()


def per_device(
    occ_size, vir_size, amplitudes, hole_integrals, particle_integrals, occ_irrep, vir_irrep, occ_energy, vir_energy
):
    width, groups = vir_size // LINES, occ_size // CORES
    p_own, q_own = amplitudes.shape
    p_all = p_own * occ_size
    bf16, f32, i32 = jnp.bfloat16, jnp.float32, jnp.int32
    dma = pltpu.SemaphoreType.DMA
    anywhere = pl.BlockSpec(memory_space=pl.ANY)
    return pl.pallas_call(
        functools.partial(kernel, width, groups),
        out_shape=jax.ShapeDtypeStruct((q_own, p_own), f32),
        in_specs=[anywhere] * 7,
        out_specs=anywhere,
        scratch_shapes=[
            pltpu.SMEM(occ_irrep.shape, i32),
            pltpu.SMEM(vir_irrep.shape, i32),
            pltpu.VMEM((1, p_all), i32),
            pltpu.VMEM((LINES, 1, q_own), i32),
            pltpu.VMEM((1, p_own), f32),
            pltpu.VMEM((1, q_own), f32),
            pltpu.VMEM((p_own, width * q_own), bf16),
            pltpu.VMEM((LINES, width * q_own, q_own), bf16),
            pltpu.VMEM((LINES, width * q_own, q_own), bf16),
            pltpu.VMEM((LINES, width - 1, q_own // CORES, q_own), bf16),
            pltpu.VMEM((p_all, q_own), bf16),
            pltpu.VMEM((p_own, p_all), bf16),
            pltpu.VMEM((p_own, q_own), f32),
            pltpu.VMEM((p_own // ROWS, q_own // HALVES), f32),
            pltpu.VMEM((LINES - 1, p_own, q_own), jnp.int16),
            pltpu.VMEM(((LINES - 1) * ROWS, 1, q_own), f32),
            pltpu.VMEM((LINES, p_own, q_own), jnp.int16),
            pltpu.VMEM((LINES * ROWS, 1, q_own), f32),
            pltpu.VMEM((q_own, p_own), f32),
            dma((width - 1, ROWS)),
            dma((width - 1, ROWS)),
            dma((width - 1, LINES, HALVES)),
            dma((width - 1, LINES, HALVES, CORES)),
            dma((width - 1, LINES, HALVES)),
            dma((occ_size - 1,)),
            dma((occ_size,)),
            dma((LINES - 1, HALVES, ROWS)),
            dma((LINES, HALVES, ROWS)),
            dma((LINES - 1, HALVES, ROWS)),
            dma((LINES, HALVES, ROWS)),
            dma((LINES, width - 1)),
            dma((LINES,)),
            dma((7,)),
            dma((HALVES, ROWS)),
        ],
        compiler_params=pltpu.CompilerParams(
            collective_id=0, has_side_effects=True, vmem_limit_bytes=60 * 1024 * 1024
        ),
    )(
        amplitudes, hole_integrals, particle_integrals, occ_irrep, vir_irrep,
        occ_energy[None, :], vir_energy[None, :],
    )


def solution(mesh):
    placed = (P("occ", "vir"), P("occ", None), P("vir", None), P(), P(), P("occ"), P("vir"))
    return jax.shard_map(
        functools.partial(per_device, mesh.shape["occ"], mesh.shape["vir"]),
        mesh=mesh, in_specs=placed, out_specs=P("vir", "occ"), check_vma=False,
    )
```

profile of v0, /device:TPU:8, one launch (start us, length us, event | category | flops | bytes accessed | tf_op | source)
XLA Modules:
  0.0 57.1 jit_solution(13211320752152247641)
XLA Ops:
  0.0 54.8 %shard_map.73 = f32[512,512]{1,0:T(8,128)} custom-call(bf16[512,512]{1,0:T(8,128)(2,1)} %amp.1, bf16[512,2048]{1,0:T(8,128)(2,1)} %hole.1, bf16[512,4096]{1,0:T(8,128)(2,1)} %slab.1, s32[32]{0:T(128)} %occ_irrep.1, s32[64]{0:T(128)} %vir_irrep.1, f32[1,512]{1,0:T(1,128)} %bitcast.2, f32[1,512]{1,0:T(1,128)} %bitcast.3), custom_call_target="tpu_custom_call" | custom-call | tf_op jit(solution)/shard_map/pallas_call | solution.py:302
  54.8 2.3 %copy.9 = f32[512,512]{1,0:T(8,128)} copy(f32[512,512]{1,0:T(8,128)} %shard_map.73) | data formatting | bytes 2097152
where the time goes:
time: 57.2 us; the launch traced here: 57.1 us
  Pallas kernels  54.8 us (96%)
  local copies, waits for them, and re-layouts  2.26 us (4%)
    pallas_call x1, Pallas kernels, per_device(): pl.pallas_call(functools.partial(kernel, width, groups), out_shape=jax.Sh...  54.8 us
    unnamed x1, local copies, waits for them, and re-layouts  2.26 us

commit v1 on v0

--- a/solution.py
+++ b/solution.py
@@ -12,20 +12,20 @@
 LINES = 4
 ROWS = 4
 HALVES = 2
+EARLY = 1
 TOP = 32000.0
 MESH = pl.DeviceIdType.MESH
-ORDER = (
-    ("t", 0), ("v", 0, 0), ("v", 0, 1), ("t", 1), ("v", 1, 0), ("t", 2), ("t", 3), ("v", 1, 1),
-    ("v", 2, 0), ("v", 2, 1), ("v", 3, 0), ("v", 3, 1),
-)
+ORDER = "ttvvttvvvv"
 
 
 def kernel(
     width, groups, amp, hole, slab, occ_irrep, vir_irrep, occ_e, vir_e, out,
     occ_tags, vir_tags, occ_labels, vir_labels, occ_row, vir_row,
-    t_all, v_all, v_masked, v_send, cols_all, hole_all, acc, tmp, box_out, scale_out, box_in, scale_in, result,
+    t_all, v_all, v_masked, v_send, v_mate, cols_all, hole_all, acc, tmp, box_out, scale_out, box_in, scale_in, result,
+    mate_labels, early_out, early_scale_out, early_in, early_scale_in, extra_in, extra_scale_in,
     t_send, t_sem, v_sends, v_sem, relay_send, pair_send, pair_sem,
     box_send, box_sem, scale_send, scale_sem, local_sem, own_sem, load_sem, out_sem,
+    mate_load, early_send, early_sem, extra_send, extra_sem,
 ):
     p_own, q_own = amp.shape
     o, v = lax.axis_index("occ"), lax.axis_index("vir")
@@ -36,13 +36,18 @@
     half = z // 2
     mid = lax.rem(z + half, 2)
     mate, far, near = z + 1 - 2 * lax.rem(z, 2), 3 * (1 - half), 2 - half
-    owner = [mid * mate + (1 - mid) * far, mid * far + (1 - mid) * near, mid * near + (1 - mid) * mate, z]
-    target = [mate, mid * far + (1 - mid) * mate, mid * near + (1 - mid) * mate]
-    box = [2 * (1 - mid), mid + 3 * (1 - mid), mid]
+    owner = [far, mid * mate + (1 - mid) * near, mid * near + (1 - mid) * mate, z]
+    target = [mid * far + (1 - mid) * mate, mate, mid * near + (1 - mid) * mate]
+    box = [2 - mid, 3 * (1 - mid), mid]
     is_mid = mid == 1
     rows, cols, share = p_own // ROWS, q_own // HALVES, q_own // CORES
     tiles = q_own // TILE
     others = range(1, width)
+    early = pl.ds(0, EARLY * rows)
+    order, count = [], {"t": 0, "v": 0}
+    for kind in ORDER + "v" * HALVES:
+        order.append((kind, count[kind]) if kind == "t" else (kind, count[kind] // HALVES, count[kind] % HALVES))
+        count[kind] += 1
 
     def xdev(k):
         return (o, z * width + lax.rem(x + k, width))
@@ -71,6 +76,10 @@
         return pl.ds(pl.multiple_of((zz * width + xx) * q_own, q_own), q_own)
 
     load("amp", amp, t_all.at[:, pl.ds(0, q_own)], load_sem.at[0])
+    load("occ_tags", occ_irrep, occ_tags, load_sem.at[1])
+    load("vir_tags", vir_irrep, vir_tags, load_sem.at[2])
+    for k in range(width):
+        load(("mate", k), slab.at[:, columns(mate, lax.rem(x + k, width))], v_mate.at[k], mate_load.at[k])
     for j in range(LINES):
         for k in others:
             load(
@@ -79,8 +88,6 @@
                 v_send.at[j, k - 1], local_sem.at[j, k - 1],
             )
         load(("own", j), slab.at[:, columns(owner[j], x)], v_all.at[j, pl.ds(0, q_own), :], own_sem.at[j])
-    load("occ_tags", occ_irrep, occ_tags, load_sem.at[1])
-    load("vir_tags", vir_irrep, vir_tags, load_sem.at[2])
     load("occ_row", occ_e, occ_row, load_sem.at[3])
     load("vir_row", vir_e, vir_row, load_sem.at[4])
     load("hole", hole, hole_all, load_sem.at[5])
@@ -115,33 +122,77 @@
             pair_send.at[d - 1], pair_sem.at[o], (lax.rem(o + d, occ_size), v),
         )
 
+    fetched = set()
+
+    def x_send(step):
+        for k in others:
+            if step[0] == "t":
+                t_copy(step[1], k).start()
+                continue
+            if (step[1], k) not in fetched:
+                fetched.add((step[1], k))
+                loads["send", step[1], k].wait()
+            v_copy(step[1], step[2], k).start()
+
     loads["amp"].wait()
-    fetched = set()
-    for step in ORDER:
-        if step[0] == "t":
-            for k in others:
-                t_copy(step[1], k).start()
-            if step[1] == 0:
-                for d in range(1, occ_size):
-                    pair_copy(d).start()
-                load("pairs", amp, cols_all.at[pl.ds(pl.multiple_of(o * p_own, p_own), p_own), :], load_sem.at[6])
-        else:
-            for k in others:
-                if (step[1], k) not in fetched:
-                    fetched.add((step[1], k))
-                    loads["send", step[1], k].wait()
-                v_copy(step[1], step[2], k).start()
+    for step in order[:-HALVES]:
+        x_send(step)
+        if step == ("t", 0):
+            for d in range(1, occ_size):
+                pair_copy(d).start()
+            load("pairs", amp, cols_all.at[pl.ds(pl.multiple_of(o * p_own, p_own), p_own), :], load_sem.at[6])
 
     loads["occ_tags"].wait()
     loads["vir_tags"].wait()
     low = lax.broadcasted_iota(jnp.int32, (1, 2 * TILE), 1) < TILE
+
+    def label(ref, j, zz, xx):
+        base = (zz * width + xx) * tiles
+
+        @pl.loop(0, tiles // 2)
+        def _(i):
+            at = pl.ds(pl.multiple_of(i * 2 * TILE, 2 * TILE), 2 * TILE)
+            ref[j, :, at] = jnp.where(low, vir_tags[base + 2 * i], vir_tags[base + 2 * i + 1])
+
+    def pack(part):
+        most = jnp.maximum(jnp.max(jnp.abs(part), axis=0, keepdims=True), 1e-30)
+        return jnp.round(part * (TOP / most)).astype(jnp.int32).astype(jnp.int16), most * (1.0 / TOP)
+
+    def early_copies(k):
+        land, where = (box_in.at[0, early, :], scale_in.at[0]) if k == 0 else (early_in.at[k - 1], early_scale_in.at[k - 1])
+        device = (o, mate * width + x)
+        return (
+            remote(early_out.at[k], land, early_send.at[0, k], early_sem.at[0, k], device),
+            remote(early_scale_out.at[k], where, early_send.at[1, k], early_sem.at[1, k], device),
+        )
+
+    def extra_copies(k):
+        return (
+            remote(early_in.at[k - 1], extra_in.at[width - k - 1], extra_send.at[0, k - 1], extra_sem.at[0, width - k - 1], xdev(k)),
+            remote(
+                early_scale_in.at[k - 1], extra_scale_in.at[width - k - 1],
+                extra_send.at[1, k - 1], extra_sem.at[1, width - k - 1], xdev(k),
+            ),
+        )
+
+    for k in reversed(range(width)):
+        label(mate_labels, k, mate, lax.rem(x + k, width))
+        loads["mate", k].wait()
+
+        @pl.loop(0, tiles)
+        def _(i):
+            part = pl.ds(pl.multiple_of(i * TILE, TILE), TILE)
+            keep = (mate_labels[k] == vir_tags[(z * width + x) * tiles + i]).astype(jnp.float32).astype(jnp.bfloat16)
+            v_mate[k, part, :] = v_mate[k, part, :] * keep
+
+        early_out[k], early_scale_out[k] = pack(
+            jnp.dot(t_all[early, pl.ds(0, q_own)], v_mate[k], preferred_element_type=jnp.float32)
+        )
+        for copy in early_copies(k):
+            copy.start()
+
     for j in range(LINES):
-        base = (owner[j] * width + x) * tiles
-
-        @pl.loop(0, tiles // 2)
-        def _(i):
-            at = pl.ds(pl.multiple_of(i * 2 * TILE, 2 * TILE), 2 * TILE)
-            vir_labels[j, :, at] = jnp.where(low, vir_tags[base + 2 * i], vir_tags[base + 2 * i + 1])
+        label(vir_labels, j, owner[j], x)
 
     @pl.loop(0, occ_tags.shape[0] // 2)
     def _(i):
@@ -192,26 +243,43 @@
 
     def unit(j, h, i):
         at, there = pl.ds(pl.multiple_of(i * rows, rows), rows), pl.ds(h * cols, cols)
-        part = jnp.dot(t_all[at, :], v_masked[j, :, there], preferred_element_type=jnp.float32)
-        if j == LINES - 1:
-            acc[at, there] += part
-            return
-        if j > 0:
-            tmp[...] = part
+
+        def product():
+            return jnp.dot(t_all[at, :], v_masked[j, :, there], preferred_element_type=jnp.float32)
+
+        def send(part):
+            box_out[j, at, there], scale_out[j * ROWS + i, :, there] = pack(part)
+            for copy in box_copies(j, h, i):
+                copy.start()
+
+        def merge(b):
+            tmp[...] = product()
 
             @pl.when(is_mid)
             def _():
-                tmp[...] += arrived(j + 1, h, i)
-
-            part = tmp[...]
-        most = jnp.maximum(jnp.max(jnp.abs(part), axis=0, keepdims=True), 1e-30)
-        box_out[j, at, there] = jnp.round(part * (TOP / most)).astype(jnp.int32).astype(jnp.int16)
-        scale_out[j * ROWS + i, :, there] = most * (1.0 / TOP)
-        for copy in box_copies(j, h, i):
-            copy.start()
+                tmp[...] += arrived(b, h, i)
+
+            send(tmp[...])
+
+        if j == LINES - 1:
+            acc[at, there] += product()
+        elif j == 0:
+            merge(2)
+        elif j == 1:
+            pl.when(jnp.logical_or(i >= EARLY, mid == 0))(lambda: send(product()))
+        else:
+            pl.when(jnp.logical_or(i >= EARLY, is_mid))(lambda: merge(3))
 
     have_t, have_v = 0, []
-    for step in ORDER:
+    for n, step in enumerate(order):
+        if n == ORDER.rindex("t") + 1:
+            for k in others:
+                landed(early_in.at[k - 1], early_sem.at[0, k])
+                landed(early_scale_in.at[k - 1], early_sem.at[1, k])
+                for copy in extra_copies(k):
+                    copy.start()
+            for last in order[-HALVES:]:
+                x_send(last)
         if step[0] == "t":
             i = step[1]
             for d in others:
@@ -253,41 +321,74 @@
 
     loads["occ_row"].wait()
     loads["vir_row"].wait()
+    for i in range(ROWS):
+        at = pl.ds(i * rows, rows)
+        result[:, at] = 1.0 / (jnp.broadcast_to(vir_row[...], (rows, q_own)).T - occ_row[:, at])
+
+    for h in range(HALVES):
+
+        @pl.loop(0, ROWS)
+        def _(i):
+            at, there = pl.ds(pl.multiple_of(i * rows, rows), rows), pl.ds(h * cols, cols)
+            acc[at, there] += arrived(1, h, i)
+
+    landed(box_in.at[0, early, :], early_sem.at[0, 0])
+    landed(scale_in.at[0], early_sem.at[1, 0])
+    acc[early, :] += box_in[0, early, :].astype(jnp.float32) * scale_in[0]
+    for d in others:
+        landed(extra_in.at[d - 1], extra_sem.at[0, d - 1])
+        landed(extra_scale_in.at[d - 1], extra_sem.at[1, d - 1])
+        acc[early, :] += extra_in[d - 1].astype(jnp.float32) * extra_scale_in[d - 1]
 
     def out_copy(h, i):
         at, there = pl.ds(pl.multiple_of(i * rows, rows), rows), pl.ds(h * cols, cols)
         return pltpu.make_async_copy(result.at[there, at], out.at[there, at], out_sem.at[h, i])
 
+    def finish(h, i, total):
+        at, there = pl.ds(pl.multiple_of(i * rows, rows), rows), pl.ds(h * cols, cols)
+        result[there, at] = total.T * result[there, at]
+        out_copy(h, i).start()
+
     for h in range(HALVES):
         there = pl.ds(h * cols, cols)
-        column = jnp.broadcast_to(vir_row[:, there], (rows, cols)).T
+        for i in range(EARLY):
+            finish(h, i, acc[pl.ds(i * rows, rows), there])
+
+        if h == HALVES - 1:
+            for d in range(1, occ_size):
+                pair_copy(d).wait_send()
+            for k in range(width):
+                for copy in early_copies(k):
+                    copy.wait_send()
+            for k in others:
+                for copy in extra_copies(k):
+                    copy.wait_send()
+                for i in range(ROWS):
+                    t_copy(i, k).wait_send()
+                for j in range(LINES):
+                    for hh in range(HALVES):
+                        v_copy(j, hh, k).wait_send()
+                        relay_copy(j, hh, k).wait_send()
+            for j in range(LINES - 1):
+                for hh in range(HALVES):
+
+                    @pl.loop(0, ROWS)
+                    def _(i):
+                        @pl.when(jnp.logical_or(i >= EARLY, jnp.logical_or(j == 0, mid == j - 1)))
+                        def _():
+                            for copy in box_copies(j, hh, i):
+                                copy.wait_send()
+
+        @pl.loop(EARLY, ROWS)
+        def _(i):
+            at = pl.ds(pl.multiple_of(i * rows, rows), rows)
+            finish(h, i, acc[at, there] + arrived(0, h, i))
+
+    for h in range(HALVES):
 
         @pl.loop(0, ROWS)
         def _(i):
-            at = pl.ds(pl.multiple_of(i * rows, rows), rows)
-            total = acc[at, there] + arrived(1, h, i)
-            total = total + arrived(0, h, i)
-            result[there, at] = total.T / (column - occ_row[:, at])
-            out_copy(h, i).start()
-
-    for h in range(HALVES):
-
-        @pl.loop(0, ROWS)
-        def _(i):
             out_copy(h, i).wait()
-            for j in range(LINES - 1):
-                for copy in box_copies(j, h, i):
-                    copy.wait_send()
-
-    for d in range(1, occ_size):
-        pair_copy(d).wait_send()
-    for k in others:
-        for i in range(ROWS):
-            t_copy(i, k).wait_send()
-        for j in range(LINES):
-            for h in range(HALVES):
-                v_copy(j, h, k).wait_send()
-                relay_copy(j, h, k).wait_send()
 
 
 def per_device(
@@ -295,7 +396,7 @@
 ):
     width, groups = vir_size // LINES, occ_size // CORES
     p_own, q_own = amplitudes.shape
-    p_all = p_own * occ_size
+    p_all, early = p_own * occ_size, EARLY * p_own // ROWS
     bf16, f32, i32 = jnp.bfloat16, jnp.float32, jnp.int32
     dma = pltpu.SemaphoreType.DMA
     anywhere = pl.BlockSpec(memory_space=pl.ANY)
@@ -315,6 +416,7 @@
             pltpu.VMEM((LINES, width * q_own, q_own), bf16),
             pltpu.VMEM((LINES, width * q_own, q_own), bf16),
             pltpu.VMEM((LINES, width - 1, q_own // CORES, q_own), bf16),
+            pltpu.VMEM((width, q_own, q_own), bf16),
             pltpu.VMEM((p_all, q_own), bf16),
             pltpu.VMEM((p_own, p_all), bf16),
             pltpu.VMEM((p_own, q_own), f32),
@@ -324,6 +426,13 @@
             pltpu.VMEM((LINES, p_own, q_own), jnp.int16),
             pltpu.VMEM((LINES * ROWS, 1, q_own), f32),
             pltpu.VMEM((q_own, p_own), f32),
+            pltpu.VMEM((width, 1, q_own), i32),
+            pltpu.VMEM((width, early, q_own), jnp.int16),
+            pltpu.VMEM((width, 1, q_own), f32),
+            pltpu.VMEM((width - 1, early, q_own), jnp.int16),
+            pltpu.VMEM((width - 1, 1, q_own), f32),
+            pltpu.VMEM((width - 1, early, q_own), jnp.int16),
+            pltpu.VMEM((width - 1, 1, q_own), f32),
             dma((width - 1, ROWS)),
             dma((width - 1, ROWS)),
             dma((width - 1, LINES, HALVES)),
@@ -339,6 +448,11 @@
             dma((LINES,)),
             dma((7,)),
             dma((HALVES, ROWS)),
+            dma((width,)),
+            dma((2, width)),
+            dma((2, width)),
+            dma((2, width - 1)),
+            dma((2, width - 1)),
         ],
         compiler_params=pltpu.CompilerParams(
             collective_id=0, has_side_effects=True, vmem_limit_bytes=60 * 1024 * 1024

time: 57.2 us -> 53.7 us (0.939)
  Pallas kernels: 54.8 us -> 51.2 us
    pallas_call x1, Pallas kernels: 54.8 us -> 51.2 us  [per_device(): pl.pallas_call(functools.partial(kernel, width, groups), out_shape=jax.Sh...]
where the time goes in v1:
time: 53.7 us; the launch traced here: 53.5 us
  Pallas kernels  51.2 us (95%)
  local copies, waits for them, and re-layouts  2.26 us (4%)
    pallas_call x1, Pallas kernels, per_device(): pl.pallas_call(functools.partial(kernel, width, groups), out_shape=jax.Sh...  51.2 us
    unnamed x1, local copies, waits for them, and re-layouts  2.26 us

profile of v1, /device:TPU:8, one launch (start us, length us, event | category | flops | bytes accessed | tf_op | source)
XLA Modules:
  0.0 53.5 jit_solution(13311141964473012223)
XLA Ops:
  0.0 51.2 %shard_map.73 = f32[512,512]{1,0:T(8,128)} custom-call(bf16[512,512]{1,0:T(8,128)(2,1)} %amp.1, bf16[512,2048]{1,0:T(8,128)(2,1)} %hole.1, bf16[512,4096]{1,0:T(8,128)(2,1)} %slab.1, s32[32]{0:T(128)} %occ_irrep.1, s32[64]{0:T(128)} %vir_irrep.1, f32[1,512]{1,0:T(1,128)} %bitcast.2, f32[1,512]{1,0:T(1,128)} %bitcast.3), custom_call_target="tpu_custom_call" | custom-call | tf_op jit(solution)/shard_map/pallas_call | solution.py:403
  51.2 2.3 %copy.9 = f32[512,512]{1,0:T(8,128)} copy(f32[512,512]{1,0:T(8,128)} %shard_map.73) | data formatting | bytes 2097152

commit v2 on v1

v2 whole, which is shorter than its diff:
```python
import functools

import jax
import jax.numpy as jnp
from jax import lax
from jax.experimental import pallas as pl
from jax.experimental.pallas import tpu as pltpu
from jax.sharding import PartitionSpec as P

TILE = 64
CORES = 2
LANES = 128
QUARTERS = 2 * CORES
LINES = 4
EIGHTHS = (3, 1, 2, 2)
ROWS = len(EIGHTHS)
PAIR_PIECES = 4
HALVES = 2
EARLY = 1
TOP = 32000.0
MESH = pl.DeviceIdType.MESH
ORDER = ("v0", "v1", "t0", "t1", "t2", "v2", "t3", "v3", "v4", "v5", "v6", "v7")
OUTER = (
    "a0", "a1", "p1", "p2", "b0", "c0", "t0", "b1", "c1", "t1", "e0", "t2", "a2", "t3", "a3", "b2",
    "c2", "a4", "q0", "a5", "a6", "b3", "c3", "a7", "p3", "b4", "c4", "q1", "b5", "q2", "c5", "b6",
    "c6", "b7", "c7", "q3", "h0",
)
INNER = (
    "a0", "a1", "p1", "p2", "b0", "c0", "t0", "b1", "c1", "t1", "e0", "t2", "a2", "m00", "m01", "t3",
    "m10", "m11", "a3", "b2", "m20", "c2", "a4", "m21", "q0", "a5", "m30", "a6", "b3", "m31", "c3", "a7",
    "p3", "b4", "c4", "q1", "b5", "m02", "q2", "m12", "c5", "b6", "m22", "c6", "b7", "m32", "c7", "q3",
    "m03", "m13", "m23", "m33", "h0",
)


def kernel(
    width, groups, amp, hole, slab, occ_irrep, vir_irrep, occ_e, vir_e, out,
    occ_tags, vir_tags, occ_labels, vir_labels, occ_row, vir_row,
    t_all, v_all, v_masked, v_send, v_mate, cols_all, hole_all, acc, box_out, scale_out, box_in, scale_in, result,
    mate_labels, early_out, early_scale_out, early_in, early_scale_in, extra_in, extra_scale_in, gauge,
    sent, t_sem, v_sem, pair_sem, box_sem, local_sem, own_sem, load_sem, out_sem, mate_load, early_sem, extra_sem,
):
    p_own, q_own = amp.shape
    o, v = lax.axis_index("occ"), lax.axis_index("vir")
    c = lax.rem(o, CORES)
    z, x = v // width, lax.rem(v, width)
    occ_size = groups * CORES
    partner = o + 1 - 2 * c
    half = z // 2
    mid = lax.rem(z + half, 2)
    mate, far, near = z + 1 - 2 * lax.rem(z, 2), 3 * (1 - half), 2 - half
    owner = [far, near, mate, z]
    target = [mid * far + (1 - mid) * mate, mid * near + (1 - mid) * mate, mate]
    box = [2 - mid, 3 - 2 * mid, 0]
    rows, cols, share = p_own // PAIR_PIECES, q_own // HALVES, q_own // QUARTERS
    starts = [sum(EIGHTHS[:i]) * p_own // 8 for i in range(ROWS + 1)]
    group, odd = o // CORES, lax.rem(o // CORES, 2)
    across = o + CORES - 2 * CORES * odd
    mine, opposite = odd * CORES + c, (1 - odd) * CORES + c
    tiles = q_own // TILE
    others = range(1, width)
    early = pl.ds(0, starts[EARLY])

    def some(i):
        return pl.ds(starts[i], starts[i + 1] - starts[i])


    def xdev(k):
        return (o, z * width + lax.rem(x + k, width))

    def remote(src, dst, send, recv, device):
        return pltpu.make_async_remote_copy(
            src_ref=src, dst_ref=dst, send_sem=send, recv_sem=recv, device_id=device, device_id_type=MESH
        )

    def landed(ref, sem):
        pltpu.make_async_copy(ref, ref, sem).wait()

    def both(height, length, sem):
        landed(gauge.at[pl.ds(0, (2 * height * length + 4 * length) // 512)], sem)

    barrier = pltpu.get_barrier_semaphore()
    peers = [(partner, v)] + [(lax.rem(o + CORES * d, occ_size), v) for d in range(1, groups)]
    peers += [xdev(k) for k in others] + [(o, mate * width + x), (o, near * width + x)]
    for peer in peers:
        pl.semaphore_signal(barrier, inc=1, device_id=peer, device_id_type=MESH)

    loads = {}

    def load(name, src, dst, sem):
        loads[name] = pltpu.make_async_copy(src, dst, sem)
        loads[name].start()

    def columns(zz, xx):
        return pl.ds(pl.multiple_of((zz * width + xx) * q_own, q_own), q_own)

    load("amp", amp, t_all.at[:, pl.ds(0, q_own)], load_sem.at[0])
    load("occ_tags", occ_irrep, occ_tags, load_sem.at[1])
    load("vir_tags", vir_irrep, vir_tags, load_sem.at[2])
    for k in range(width):
        load(("mate", k), slab.at[:, columns(mate, lax.rem(x + k, width))], v_mate.at[k], mate_load.at[k])
    for j in range(LINES):
        for k in others:
            load(
                ("send", j, k),
                slab.at[pl.ds(pl.multiple_of(mine * share, share), share), columns(owner[j], lax.rem(x + k, width))],
                v_send.at[j, k - 1], local_sem.at[j, k - 1],
            )
        load(("own", j), slab.at[:, columns(owner[j], x)], v_all.at[j, pl.ds(0, q_own), :], own_sem.at[j])
    load("occ_row", occ_e, occ_row, load_sem.at[3])
    load("vir_row", vir_e, vir_row, load_sem.at[4])
    load("hole", hole, hole_all, load_sem.at[5])

    pl.semaphore_wait(barrier, len(peers) - 1 + 2 * mid)

    def t_copy(i, k):
        at = some(i)
        return remote(
            t_all.at[at, pl.ds(0, q_own)], t_all.at[at, pl.ds((width - k) * q_own, q_own)],
            sent.at[0], t_sem.at[width - k - 1, i], xdev(k),
        )

    def v_piece(j, h, d, quarter):
        return v_all.at[
            j, pl.ds(pl.multiple_of(d * q_own + quarter * share, share), share), pl.ds(h * cols, cols)
        ]

    def v_copy(j, h, k):
        return remote(
            v_send.at[j, k - 1, :, pl.ds(h * cols, cols)], v_piece(j, h, width - k, mine),
            sent.at[1], v_sem.at[width - k - 1, j, h, mine], xdev(k),
        )

    def relay_copies(j, h, d, first=True, second=True):
        piece, sem = v_piece(j, h, d, mine), v_sem.at[d - 1, j, h, mine]
        other, other_sem = v_piece(j, h, d, opposite), v_sem.at[d - 1, j, h, opposite]
        copies = []
        if first:
            copies.append(remote(piece, piece, sent.at[2], sem, (across, v)))
            copies.append(remote(piece, piece, sent.at[3], sem, (partner, v)))
        if second:
            copies.append(remote(other, other, sent.at[4], other_sem, (partner, v)))
        return copies

    def pair_rows(oo, i):
        return cols_all.at[pl.ds(pl.multiple_of(oo * p_own + i * rows, rows), rows), :]

    def pair_copy(i, d):
        device = partner if d == 0 else lax.rem(o + CORES * d, occ_size)
        return remote(
            t_all.at[pl.ds(i * rows, rows), pl.ds(0, q_own)], pair_rows(o, i), sent.at[5], pair_sem.at[o, i], (device, v)
        )

    def pass_copy(i, d):
        oo = lax.rem(o + CORES * d, occ_size)
        return remote(pair_rows(oo, i), pair_rows(oo, i), sent.at[6], pair_sem.at[oo, i], (partner, v))

    fetched = set()

    def x_send(kind, n):
        for k in others:
            if kind == "t":
                t_copy(n, k).start()
                continue
            j, h = divmod(n, HALVES)
            if (j, k) not in fetched:
                fetched.add((j, k))
                loads["send", j, k].wait()
            v_copy(j, h, k).start()

    loads["amp"].wait()
    for step in ORDER:
        x_send(step[0], int(step[1:]))
        if step == "t0":
            for d in range(1, groups):
                pair_copy(0, d).start()
    for i in range(PAIR_PIECES):
        pair_copy(i, 0).start()
    load("pairs", amp, cols_all.at[pl.ds(pl.multiple_of(o * p_own, p_own), p_own), :], load_sem.at[6])

    loads["occ_tags"].wait()
    loads["vir_tags"].wait()
    low = lax.broadcasted_iota(jnp.int32, (1, 2 * TILE), 1) < TILE

    def label(ref, j, zz, xx):
        base = (zz * width + xx) * tiles

        @pl.loop(0, tiles // 2)
        def _(i):
            at = pl.ds(pl.multiple_of(i * 2 * TILE, 2 * TILE), 2 * TILE)
            ref[j, :, at] = jnp.where(low, vir_tags[base + 2 * i], vir_tags[base + 2 * i + 1])

    def pack(part):
        most = jnp.maximum(jnp.max(jnp.abs(part), axis=0, keepdims=True), 1e-30)
        return jnp.round(part * (TOP / most)).astype(jnp.int32).astype(jnp.int16), most * (1.0 / TOP)

    def early_copies(k):
        land, where = (box_in.at[0, early, :], scale_in.at[0]) if k == 0 else (early_in.at[k - 1], early_scale_in.at[k - 1])
        device = (o, mate * width + x)
        return (
            remote(early_out.at[k], land, sent.at[7], early_sem.at[0, k], device),
            remote(early_scale_out.at[k], where, sent.at[8], early_sem.at[0, k], device),
        )

    def extra_copies(k):
        return (
            remote(early_in.at[k - 1], extra_in.at[width - k - 1], sent.at[9], extra_sem.at[0, width - k - 1], xdev(k)),
            remote(
                early_scale_in.at[k - 1], extra_scale_in.at[width - k - 1],
                sent.at[10], extra_sem.at[0, width - k - 1], xdev(k),
            ),
        )

    for k in reversed(range(width)):
        label(mate_labels, k, mate, lax.rem(x + k, width))
        loads["mate", k].wait()

        @pl.loop(0, tiles)
        def _(i):
            part = pl.ds(pl.multiple_of(i * TILE, TILE), TILE)
            keep = (mate_labels[k] == vir_tags[(z * width + x) * tiles + i]).astype(jnp.float32).astype(jnp.bfloat16)
            v_mate[k, part, :] = v_mate[k, part, :] * keep

        early_out[k], early_scale_out[k] = pack(
            jnp.dot(t_all[early, pl.ds(0, q_own)], v_mate[k], preferred_element_type=jnp.float32)
        )
        for copy in early_copies(k):
            copy.start()

    for j in range(LINES):
        label(vir_labels, j, owner[j], x)

    @pl.loop(0, occ_tags.shape[0] // 2)
    def _(i):
        at = pl.ds(pl.multiple_of(i * 2 * TILE, 2 * TILE), 2 * TILE)
        occ_labels[:, at] = jnp.where(low, occ_tags[2 * i], occ_tags[2 * i + 1])

    def mask(j, d, at):
        first = (z * width + lax.rem(x + d, width)) * tiles
        labels = vir_labels[j, :, at]

        @pl.loop(0, tiles)
        def _(i):
            part = pl.ds(pl.multiple_of(d * q_own + i * TILE, TILE), TILE)
            keep = (labels == vir_tags[first + i]).astype(jnp.float32).astype(jnp.bfloat16)
            v_masked[j, part, at] = v_all[j, part, at] * keep

    everything = pl.ds(0, q_own)
    loads["own", 0].wait()
    mask(0, 0, everything)

    loads["hole"].wait()

    @pl.loop(0, p_own // TILE)
    def _(i):
        at = pl.ds(pl.multiple_of(i * TILE, TILE), TILE)
        keep = (occ_labels[...] == occ_tags[o * (p_own // TILE) + i]).astype(jnp.float32).astype(jnp.bfloat16)
        hole_all[at, :] = hole_all[at, :] * keep

    def box_copies(j, h, i):
        at, there = some(i), pl.ds(h * cols, cols)
        device = (o, target[j] * width + x)
        return (
            remote(
                box_out.at[j, at, there], box_in.at[box[j], at, there],
                sent.at[11 + j // 2], box_sem.at[box[j], h, i], device,
            ),
            remote(
                scale_out.at[j * ROWS + i, :, there], scale_in.at[box[j] * ROWS + i, :, there],
                sent.at[13 + j // 2], box_sem.at[box[j], h, i], device,
            ),
        )

    def arrived(b, h, i):
        at, there = some(i), pl.ds(h * cols, cols)
        both(starts[i + 1] - starts[i], cols, box_sem.at[b, h, i])
        return box_in[b, at, there].astype(jnp.float32) * scale_in[b * ROWS + i, :, there]

    def unit(j, h, i, merge=False):
        at, there = some(i), pl.ds(h * cols, cols)
        part = jnp.dot(t_all[at, :], v_masked[j, :, there], preferred_element_type=jnp.float32)
        if j == LINES - 1:
            acc[at, there] = part
            return
        if merge:
            part = part + arrived(j + 2, h, i)
        box_out[j, at, there], scale_out[j * ROWS + i, :, there] = pack(part)
        for copy in box_copies(j, h, i):
            copy.start()

    def skipped(j, i, inner):
        return (inner and j < LINES - 2) or (j == LINES - 2 and i < EARLY)

    def act(kind, n, i, inner, have_t, have_v):
        j, h = divmod(n, HALVES)
        if kind == "t":
            for d in others:
                landed(t_all.at[some(n), pl.ds(d * q_own, q_own)], t_sem.at[d - 1, n])
            have_t.append(n)
            for jj, hh in have_v:
                if not skipped(jj, n, inner):
                    unit(jj, hh, n)
        elif kind == "a":
            for d in others:
                landed(v_piece(j, h, d, mine), v_sem.at[d - 1, j, h, mine])
                for copy in relay_copies(j, h, d, second=False):
                    copy.start()
        elif kind == "b":
            for d in others:
                landed(v_piece(j, h, d, opposite), v_sem.at[d - 1, j, h, opposite])
                relay_copies(j, h, d, first=False)[0].start()
            if h == 0 and j > 0:
                loads["own", j].wait()
                mask(j, 0, everything)
        elif kind == "c":
            for d in others:
                for odds in (odd, 1 - odd):
                    quarter = odds * CORES + 1 - c
                    landed(v_piece(j, h, d, quarter), v_sem.at[d - 1, j, h, quarter])
                mask(j, d, pl.ds(h * cols, cols))
            have_v.append((j, h))
            for t in have_t:
                if not skipped(j, t, inner):
                    unit(j, h, t)
        elif kind == "m":
            unit(j, h, i, merge=True)
        elif kind == "p":
            for d in range(1, groups):
                pair_copy(n, d).start()
        elif kind == "q":
            for d in range(1, groups):
                oo = lax.rem(o + CORES * d, occ_size)
                landed(pair_rows(oo, n), pair_sem.at[oo, n])
                pass_copy(n, d).start()
        elif kind == "e":
            for k in others:
                both(starts[EARLY], q_own, early_sem.at[0, k])
                for copy in extra_copies(k):
                    copy.start()
        else:
            loads["pairs"].wait()
            for d in range(groups):
                oo = lax.rem(partner + CORES * d, occ_size)
                for i in range(PAIR_PIECES):
                    landed(pair_rows(oo, i), pair_sem.at[oo, i])

            @pl.loop(0, PAIR_PIECES)
            def _(i):
                at = pl.ds(pl.multiple_of(i * rows, rows), rows)
                acc[at, :] += jnp.dot(hole_all[at, :], cols_all[...], preferred_element_type=jnp.float32)

    def run(actions, inner):
        have_t, have_v = [], []
        for action in actions:
            act(action[0], int(action[-1]), int(action[1]), inner, have_t, have_v)

    pl.when(mid == 0)(lambda: run(OUTER, False))
    pl.when(mid == 1)(lambda: run(INNER, True))
    loads["occ_row"].wait()
    loads["vir_row"].wait()
    for i in range(PAIR_PIECES):
        at = pl.ds(i * rows, rows)
        result[:, at] = 1.0 / (jnp.broadcast_to(vir_row[...], (rows, q_own)).T - occ_row[:, at])

    for h in range(HALVES):
        for i in range(ROWS):
            acc[some(i), pl.ds(h * cols, cols)] += arrived(1, h, i)

    both(starts[EARLY], q_own, early_sem.at[0, 0])
    acc[early, :] += box_in[0, early, :].astype(jnp.float32) * scale_in[0]
    for d in others:
        both(starts[EARLY], q_own, extra_sem.at[0, d - 1])
        acc[early, :] += extra_in[d - 1].astype(jnp.float32) * extra_scale_in[d - 1]

    ends = [0] + [i + 1 for i in range(ROWS) if starts[i + 1] % LANES == 0]
    spans = list(zip(ends[:-1], ends[1:]))

    def span(first, last):
        return pl.ds(starts[first], starts[last] - starts[first])

    def out_copy(h, first, last):
        at, there = span(first, last), pl.ds(h * cols, cols)
        return pltpu.make_async_copy(result.at[there, at], out.at[there, at], out_sem.at[0])

    for h in range(HALVES):
        there = pl.ds(h * cols, cols)
        if h == HALVES - 1:
            for n, ref in enumerate((
                t_all.at[:, pl.ds(0, (width - 1) * q_own)], v_send, v_send, v_send, v_send,
                cols_all.at[pl.ds(0, groups * p_own), :], cols_all.at[pl.ds(0, (groups - 1) * p_own), :],
                early_out, early_scale_out, early_in, early_scale_in,
                box_out.at[pl.ds(0, LINES - 2)], box_out.at[LINES - 2, pl.ds(starts[EARLY], p_own - starts[EARLY]), :],
                scale_out.at[pl.ds(0, (LINES - 2) * ROWS)],
                scale_out.at[pl.ds((LINES - 2) * ROWS + EARLY, ROWS - EARLY)],
            )):
                landed(ref, sent.at[n])

        for first, last in spans:
            for i in range(max(first, EARLY), last):
                acc[some(i), there] += arrived(0, h, i)
            at = span(first, last)
            result[there, at] = acc[at, there].T * result[there, at]
            out_copy(h, first, last).start()

    landed(result, out_sem.at[0])


def per_device(
    occ_size, vir_size, amplitudes, hole_integrals, particle_integrals, occ_irrep, vir_irrep, occ_energy, vir_energy
):
    width, groups = vir_size // LINES, occ_size // CORES
    p_own, q_own = amplitudes.shape
    p_all, early = p_own * occ_size, sum(EIGHTHS[:EARLY]) * p_own // 8
    bf16, f32, i32 = jnp.bfloat16, jnp.float32, jnp.int32
    dma = pltpu.SemaphoreType.DMA
    anywhere = pl.BlockSpec(memory_space=pl.ANY)
    return pl.pallas_call(
        functools.partial(kernel, width, groups),
        out_shape=jax.ShapeDtypeStruct((q_own, p_own), f32),
        in_specs=[anywhere] * 7,
        out_specs=anywhere,
        scratch_shapes=[
            pltpu.SMEM(occ_irrep.shape, i32),
            pltpu.SMEM(vir_irrep.shape, i32),
            pltpu.VMEM((1, p_all), i32),
            pltpu.VMEM((LINES, 1, q_own), i32),
            pltpu.VMEM((1, p_own), f32),
            pltpu.VMEM((1, q_own), f32),
            pltpu.VMEM((p_own, width * q_own), bf16),
            pltpu.VMEM((LINES, width * q_own, q_own), bf16),
            pltpu.VMEM((LINES, width * q_own, q_own), bf16),
            pltpu.VMEM((LINES, width - 1, q_own // QUARTERS, q_own), bf16),
            pltpu.VMEM((width, q_own, q_own), bf16),
            pltpu.VMEM((p_all, q_own), bf16),
            pltpu.VMEM((p_own, p_all), bf16),
            pltpu.VMEM((p_own, q_own), f32),
            pltpu.VMEM((LINES - 1, p_own, q_own), jnp.int16),
            pltpu.VMEM(((LINES - 1) * ROWS, 1, q_own), f32),
            pltpu.VMEM((LINES, p_own, q_own), jnp.int16),
            pltpu.VMEM((LINES * ROWS, 1, q_own), f32),
            pltpu.VMEM((q_own, p_own), f32),
            pltpu.VMEM((width, 1, q_own), i32),
            pltpu.VMEM((width, early, q_own), jnp.int16),
            pltpu.VMEM((width, 1, q_own), f32),
            pltpu.VMEM((width - 1, early, q_own), jnp.int16),
            pltpu.VMEM((width - 1, 1, q_own), f32),
            pltpu.VMEM((width - 1, early, q_own), jnp.int16),
            pltpu.VMEM((width - 1, 1, q_own), f32),
            pltpu.VMEM(((2 * p_own * q_own + 4 * q_own) // 512, 1, LANES), f32),
            dma((15,)),
            dma((width - 1, ROWS)),
            dma((width - 1, LINES, HALVES, QUARTERS)),
            dma((occ_size, PAIR_PIECES)),
            dma((LINES, HALVES, ROWS)),
            dma((LINES, width - 1)),
            dma((LINES,)),
            dma((7,)),
            dma((1,)),
            dma((width,)),
            dma((1, width)),
            dma((1, width - 1)),
        ],
        compiler_params=pltpu.CompilerParams(
            collective_id=0, has_side_effects=True, vmem_limit_bytes=60 * 1024 * 1024
        ),
    )(
        amplitudes, hole_integrals, particle_integrals, occ_irrep, vir_irrep,
        occ_energy[None, :], vir_energy[None, :],
    )


def solution(mesh):
    placed = (P("occ", "vir"), P("occ", None), P("vir", None), P(), P(), P("occ"), P("vir"))
    return jax.shard_map(
        functools.partial(per_device, mesh.shape["occ"], mesh.shape["vir"]),
        mesh=mesh, in_specs=placed, out_specs=P("vir", "occ"), check_vma=False,
    )
```

time: 53.7 us -> 49 us (0.912)
  Pallas kernels: 51.2 us -> 46.6 us
    pallas_call x1, Pallas kernels: 51.2 us -> 46.6 us  [per_device(): pl.pallas_call(functools.partial(kernel, width, groups), out_shape=jax.Sh...]
where the time goes in v2:
time: 49 us; the launch traced here: 48.9 us
  Pallas kernels  46.6 us (95%)
  local copies, waits for them, and re-layouts  2.26 us (5%)
    pallas_call x1, Pallas kernels, per_device(): pl.pallas_call(functools.partial(kernel, width, groups), out_shape=jax.Sh...  46.6 us
    unnamed x1, local copies, waits for them, and re-layouts  2.26 us

profile of v2, /device:TPU:8, one launch (start us, length us, event | category | flops | bytes accessed | tf_op | source)
XLA Modules:
  0.0 48.9 jit_solution(8126108501940074854)
XLA Ops:
  0.0 46.6 %shard_map.73 = f32[512,512]{1,0:T(8,128)} custom-call(bf16[512,512]{1,0:T(8,128)(2,1)} %amp.1, bf16[512,2048]{1,0:T(8,128)(2,1)} %hole.1, bf16[512,4096]{1,0:T(8,128)(2,1)} %slab.1, s32[32]{0:T(128)} %occ_irrep.1, s32[64]{0:T(128)} %vir_irrep.1, f32[1,512]{1,0:T(1,128)} %bitcast.2, f32[1,512]{1,0:T(1,128)} %bitcast.3), custom_call_target="tpu_custom_call" | custom-call | tf_op jit(solution)/shard_map/pallas_call | solution.py:417
  46.6 2.3 %copy.9 = f32[512,512]{1,0:T(8,128)} copy(f32[512,512]{1,0:T(8,128)} %shard_map.73) | data formatting | bytes 2097152

commit v3 on v2

--- a/solution.py
+++ b/solution.py
@@ -21,15 +21,15 @@
 MESH = pl.DeviceIdType.MESH
 ORDER = ("v0", "v1", "t0", "t1", "t2", "v2", "t3", "v3", "v4", "v5", "v6", "v7")
 OUTER = (
-    "a0", "a1", "p1", "p2", "b0", "c0", "t0", "b1", "c1", "t1", "e0", "t2", "a2", "t3", "a3", "b2",
-    "c2", "a4", "q0", "a5", "a6", "b3", "c3", "a7", "p3", "b4", "c4", "q1", "b5", "q2", "c5", "b6",
-    "c6", "b7", "c7", "q3", "h0",
+    "a0", "a1", "b0", "g0", "c0", "p1", "t0", "b1", "c1", "t1", "e0", "t2", "p2", "a2", "t3", "a3",
+    "b2", "r0", "c2", "a4", "q0", "a5", "a6", "b3", "c3", "a7", "p3", "b4", "c4", "q1", "q2", "b5",
+    "c5", "b6", "c6", "b7", "c7", "q3", "h0",
 )
 INNER = (
-    "a0", "a1", "p1", "p2", "b0", "c0", "t0", "b1", "c1", "t1", "e0", "t2", "a2", "m00", "m01", "t3",
-    "m10", "m11", "a3", "b2", "m20", "c2", "a4", "m21", "q0", "a5", "m30", "a6", "b3", "m31", "c3", "a7",
-    "p3", "b4", "c4", "q1", "b5", "m02", "q2", "m12", "c5", "b6", "m22", "c6", "b7", "m32", "c7", "q3",
-    "m03", "m13", "m23", "m33", "h0",
+    "a0", "a1", "b0", "g0", "c0", "p1", "t0", "b1", "m00", "c1", "t1", "m01", "m10", "e0", "m11", "t2",
+    "p2", "m20", "a2", "m21", "t3", "m30", "m31", "a3", "b2", "r0", "c2", "a4", "m02", "q0", "m12", "a5",
+    "m22", "a6", "b3", "m32", "c3", "a7", "p3", "b4", "c4", "q1", "q2", "b5", "m03", "m13", "c5", "b6",
+    "m23", "c6", "b7", "m33", "c7", "q3", "h0",
 )
 
 
@@ -280,7 +280,7 @@
         at, there = some(i), pl.ds(h * cols, cols)
         part = jnp.dot(t_all[at, :], v_masked[j, :, there], preferred_element_type=jnp.float32)
         if j == LINES - 1:
-            acc[at, there] = part
+            acc[at, there] += part
             return
         if merge:
             part = part + arrived(j + 2, h, i)
@@ -337,17 +337,32 @@
                 both(starts[EARLY], q_own, early_sem.at[0, k])
                 for copy in extra_copies(k):
                     copy.start()
-        else:
+        elif kind == "g":
             loads["pairs"].wait()
-            for d in range(groups):
+            for i in range(PAIR_PIECES):
+                landed(pair_rows(partner, i), pair_sem.at[partner, i])
+            pairs_product(group, False)
+        elif kind == "h":
+            for d in range(1, groups):
                 oo = lax.rem(partner + CORES * d, occ_size)
                 for i in range(PAIR_PIECES):
                     landed(pair_rows(oo, i), pair_sem.at[oo, i])
-
-            @pl.loop(0, PAIR_PIECES)
-            def _(i):
-                at = pl.ds(pl.multiple_of(i * rows, rows), rows)
-                acc[at, :] += jnp.dot(hole_all[at, :], cols_all[...], preferred_element_type=jnp.float32)
+                pairs_product(lax.rem(group + d, groups), True)
+        else:
+            loads["occ_row"].wait()
+            loads["vir_row"].wait()
+            for i in range(PAIR_PIECES):
+                at = pl.ds(i * rows, rows)
+                result[:, at] = 1.0 / (jnp.broadcast_to(vir_row[...], (rows, q_own)).T - occ_row[:, at])
+
+    def pairs_product(g, more):
+        both_cores = pl.ds(pl.multiple_of(g * CORES * p_own, CORES * p_own), CORES * p_own)
+
+        @pl.loop(0, PAIR_PIECES)
+        def _(i):
+            at = pl.ds(pl.multiple_of(i * rows, rows), rows)
+            part = jnp.dot(hole_all[at, both_cores], cols_all[both_cores, :], preferred_element_type=jnp.float32)
+            acc[at, :] = acc[at, :] + part if more else part
 
     def run(actions, inner):
         have_t, have_v = [], []
@@ -356,12 +371,6 @@
 
     pl.when(mid == 0)(lambda: run(OUTER, False))
     pl.when(mid == 1)(lambda: run(INNER, True))
-    loads["occ_row"].wait()
-    loads["vir_row"].wait()
-    for i in range(PAIR_PIECES):
-        at = pl.ds(i * rows, rows)
-        result[:, at] = 1.0 / (jnp.broadcast_to(vir_row[...], (rows, q_own)).T - occ_row[:, at])
-
     for h in range(HALVES):
         for i in range(ROWS):
             acc[some(i), pl.ds(h * cols, cols)] += arrived(1, h, i)

time: 49 us -> 48.5 us (0.990); the launches traced: 48.9 us -> 47.5 us
  Pallas kernels: 46.6 us -> 45.2 us
    pallas_call x1, Pallas kernels: 46.6 us -> 45.2 us  [per_device(): pl.pallas_call(functools.partial(kernel, width, groups), out_shape=jax.Sh...]
where the time goes in v3:
time: 48.5 us; the launch traced here: 47.5 us
  Pallas kernels  45.2 us (93%)
  local copies, waits for them, and re-layouts  2.26 us (5%)
    pallas_call x1, Pallas kernels, per_device(): pl.pallas_call(functools.partial(kernel, width, groups), out_shape=jax.Sh...  45.2 us
    unnamed x1, local copies, waits for them, and re-layouts  2.26 us

profile of v3, /device:TPU:8, one launch (start us, length us, event | category | flops | bytes accessed | tf_op | source)
XLA Modules:
  0.0 47.5 jit_solution(6219578604715301142)
XLA Ops:
  0.0 45.2 %shard_map.73 = f32[512,512]{1,0:T(8,128)} custom-call(bf16[512,512]{1,0:T(8,128)(2,1)} %amp.1, bf16[512,2048]{1,0:T(8,128)(2,1)} %hole.1, bf16[512,4096]{1,0:T(8,128)(2,1)} %slab.1, s32[32]{0:T(128)} %occ_irrep.1, s32[64]{0:T(128)} %vir_irrep.1, f32[1,512]{1,0:T(1,128)} %bitcast.2, f32[1,512]{1,0:T(1,128)} %bitcast.3), custom_call_target="tpu_custom_call" | custom-call | tf_op jit(solution)/shard_map/pallas_call | solution.py:426
  45.2 2.3 %copy.9 = f32[512,512]{1,0:T(8,128)} copy(f32[512,512]{1,0:T(8,128)} %shard_map.73) | data formatting | bytes 2097152

commit v4 on v3

--- a/solution.py
+++ b/solution.py
@@ -38,7 +38,7 @@
     occ_tags, vir_tags, occ_labels, vir_labels, occ_row, vir_row,
     t_all, v_all, v_masked, v_send, v_mate, cols_all, hole_all, acc, box_out, scale_out, box_in, scale_in, result,
     mate_labels, early_out, early_scale_out, early_in, early_scale_in, extra_in, extra_scale_in, gauge,
-    sent, t_sem, v_sem, pair_sem, box_sem, local_sem, own_sem, load_sem, out_sem, mate_load, early_sem, extra_sem,
+    sent, t_sem, v_sem, pair_sem, pass_sem, box_sem, local_sem, own_sem, load_sem, out_sem, mate_load, early_sem, extra_sem,
 ):
     p_own, q_own = amp.shape
     o, v = lax.axis_index("occ"), lax.axis_index("vir")
@@ -128,32 +128,32 @@
     def v_copy(j, h, k):
         return remote(
             v_send.at[j, k - 1, :, pl.ds(h * cols, cols)], v_piece(j, h, width - k, mine),
-            sent.at[1], v_sem.at[width - k - 1, j, h, mine], xdev(k),
+            sent.at[1], v_sem.at[width - k - 1, j, h, 0], xdev(k),
         )
 
     def relay_copies(j, h, d, first=True, second=True):
-        piece, sem = v_piece(j, h, d, mine), v_sem.at[d - 1, j, h, mine]
-        other, other_sem = v_piece(j, h, d, opposite), v_sem.at[d - 1, j, h, opposite]
+        piece, sems = v_piece(j, h, d, mine), v_sem.at[d - 1, j, h]
+        other = v_piece(j, h, d, opposite)
         copies = []
         if first:
-            copies.append(remote(piece, piece, sent.at[2], sem, (across, v)))
-            copies.append(remote(piece, piece, sent.at[3], sem, (partner, v)))
+            copies.append(remote(piece, piece, sent.at[2], sems.at[1], (across, v)))
+            copies.append(remote(piece, piece, sent.at[3], sems.at[2], (partner, v)))
         if second:
-            copies.append(remote(other, other, sent.at[4], other_sem, (partner, v)))
+            copies.append(remote(other, other, sent.at[4], sems.at[2], (partner, v)))
         return copies
 
     def pair_rows(oo, i):
         return cols_all.at[pl.ds(pl.multiple_of(oo * p_own + i * rows, rows), rows), :]
 
     def pair_copy(i, d):
-        device = partner if d == 0 else lax.rem(o + CORES * d, occ_size)
+        device = lax.rem(o + CORES * d, occ_size)
         return remote(
-            t_all.at[pl.ds(i * rows, rows), pl.ds(0, q_own)], pair_rows(o, i), sent.at[5], pair_sem.at[o, i], (device, v)
+            t_all.at[pl.ds(i * rows, rows), pl.ds(0, q_own)], pair_rows(o, i), sent.at[5], pair_sem.at[groups - d - 1, i], (device, v)
         )
 
     def pass_copy(i, d):
         oo = lax.rem(o + CORES * d, occ_size)
-        return remote(pair_rows(oo, i), pair_rows(oo, i), sent.at[6], pair_sem.at[oo, i], (partner, v))
+        return remote(pair_rows(oo, i), pair_rows(oo, i), sent.at[6], pass_sem.at[d], (partner, v))
 
     fetched = set()
 
@@ -174,8 +174,8 @@
         if step == "t0":
             for d in range(1, groups):
                 pair_copy(0, d).start()
-    for i in range(PAIR_PIECES):
-        pair_copy(i, 0).start()
+    own_pairs = pl.ds(pl.multiple_of(o * p_own, p_own), p_own)
+    remote(t_all.at[:, pl.ds(0, q_own)], cols_all.at[own_pairs, :], sent.at[5], pass_sem.at[0], (partner, v)).start()
     load("pairs", amp, cols_all.at[pl.ds(pl.multiple_of(o * p_own, p_own), p_own), :], load_sem.at[6])
 
     loads["occ_tags"].wait()
@@ -302,21 +302,19 @@
                     unit(jj, hh, n)
         elif kind == "a":
             for d in others:
-                landed(v_piece(j, h, d, mine), v_sem.at[d - 1, j, h, mine])
+                landed(v_piece(j, h, d, mine), v_sem.at[d - 1, j, h, 0])
                 for copy in relay_copies(j, h, d, second=False):
                     copy.start()
         elif kind == "b":
             for d in others:
-                landed(v_piece(j, h, d, opposite), v_sem.at[d - 1, j, h, opposite])
+                landed(v_piece(j, h, d, opposite), v_sem.at[d - 1, j, h, 1])
                 relay_copies(j, h, d, first=False)[0].start()
             if h == 0 and j > 0:
                 loads["own", j].wait()
                 mask(j, 0, everything)
         elif kind == "c":
             for d in others:
-                for odds in (odd, 1 - odd):
-                    quarter = odds * CORES + 1 - c
-                    landed(v_piece(j, h, d, quarter), v_sem.at[d - 1, j, h, quarter])
+                landed(gauge.at[pl.ds(0, 4 * share * cols // 512)], v_sem.at[d - 1, j, h, 2])
                 mask(j, d, pl.ds(h * cols, cols))
             have_v.append((j, h))
             for t in have_t:
@@ -330,7 +328,7 @@
         elif kind == "q":
             for d in range(1, groups):
                 oo = lax.rem(o + CORES * d, occ_size)
-                landed(pair_rows(oo, n), pair_sem.at[oo, n])
+                landed(pair_rows(oo, n), pair_sem.at[d - 1, n])
                 pass_copy(n, d).start()
         elif kind == "e":
             for k in others:
@@ -339,14 +337,11 @@
                     copy.start()
         elif kind == "g":
             loads["pairs"].wait()
-            for i in range(PAIR_PIECES):
-                landed(pair_rows(partner, i), pair_sem.at[partner, i])
+            landed(cols_all.at[pl.ds(0, p_own), :], pass_sem.at[0])
             pairs_product(group, False)
         elif kind == "h":
             for d in range(1, groups):
-                oo = lax.rem(partner + CORES * d, occ_size)
-                for i in range(PAIR_PIECES):
-                    landed(pair_rows(oo, i), pair_sem.at[oo, i])
+                landed(cols_all.at[pl.ds(0, p_own), :], pass_sem.at[d])
                 pairs_product(lax.rem(group + d, groups), True)
         else:
             loads["occ_row"].wait()
@@ -458,8 +453,9 @@
             pltpu.VMEM(((2 * p_own * q_own + 4 * q_own) // 512, 1, LANES), f32),
             dma((15,)),
             dma((width - 1, ROWS)),
-            dma((width - 1, LINES, HALVES, QUARTERS)),
-            dma((occ_size, PAIR_PIECES)),
+            dma((width - 1, LINES, HALVES, 3)),
+            dma((groups - 1, PAIR_PIECES)),
+            dma((groups,)),
             dma((LINES, HALVES, ROWS)),
             dma((LINES, width - 1)),
             dma((LINES,)),

time: 48.5 us -> 48.3 us (level)
  the two profiles are of different devices: /device:TPU:8 before, /device:TPU:17 now
where the time goes in v4:
time: 48.3 us; the launch traced here: 48.1 us
  Pallas kernels  45.9 us (95%)
  local copies, waits for them, and re-layouts  2.26 us (5%)
    pallas_call x1, Pallas kernels, per_device(): pl.pallas_call(functools.partial(kernel, width, groups), out_shape=jax.Sh...  45.9 us
    unnamed x1, local copies, waits for them, and re-layouts  2.26 us

profile of v4, /device:TPU:17, one launch (start us, length us, event | category | flops | bytes accessed | tf_op | source)
XLA Modules:
  0.0 48.1 jit_solution(3594433812730892431)
XLA Ops:
  0.0 45.9 %shard_map.73 = f32[512,512]{1,0:T(8,128)} custom-call(bf16[512,512]{1,0:T(8,128)(2,1)} %amp.1, bf16[512,2048]{1,0:T(8,128)(2,1)} %hole.1, bf16[512,4096]{1,0:T(8,128)(2,1)} %slab.1, s32[32]{0:T(128)} %occ_irrep.1, s32[64]{0:T(128)} %vir_irrep.1, f32[1,512]{1,0:T(1,128)} %bitcast.2, f32[1,512]{1,0:T(1,128)} %bitcast.3), custom_call_target="tpu_custom_call" | custom-call | tf_op jit(solution)/shard_map/pallas_call | solution.py:421
  45.9 2.3 %copy.9 = f32[512,512]{1,0:T(8,128)} copy(f32[512,512]{1,0:T(8,128)} %shard_map.73) | data formatting | bytes 2097152
